TPU v7x, 256 devices: a whole 4x4x8 slice. The times are simulated.
256 devices in a mesh: dp: 4 (over x), expert: 64 (over z, y, core).
Axes of the slice: x: 4, y: 4, z: 8, core: 2. Of those that a mesh axis runs over, the one named last changes fastest.
Arguments:
- tokens: bfloat16 [32768, 2048], P(('dp', 'expert')), may hold values from -6 to 6
- expert_ids: int32 [32768, 2], P(('dp', 'expert')), may hold values from 0 to 63, all different within a row; in each aligned block of 128 rows (0 to 127, 128 to 255, ...) at most 5 rows name the same one
- gate_units: int32 [32768, 2], P(('dp', 'expert')), may hold values from 64 to 1023
- capacity: int32 [64], replicated, may hold values from 512 to 1535
- w_gate: bfloat16 [64, 2048, 1408], P('expert', None, 'dp'), may hold values from -0.125 to 0.125
- w_up: bfloat16 [64, 2048, 1408], P('expert', None, 'dp'), may hold values from -0.125 to 0.125
- w_down: bfloat16 [64, 2048, 1408], P('expert', None, 'dp'), may hold values from -0.15625 to 0.15625
Outputs:
- mixed: bfloat16 [32768, 2048], P(('dp', 'expert'))
Inputs may be any that keep to these rules, and one draw needn't show every extreme that they name: `expert_ids`: each row names two different experts; of one device's 128 rows (aligned blocks) no expert is named more than 5 times.
All inputs are finite; a program needn't handle non-finite values.
Results may differ from a plain program's by a relative error of at most 0.0057.
Values may be sent and summed in bfloat16 or wider, within the bound.
A program may use at most 128 MiB of HBM per device.

v0:
```python
import jax
import jax.numpy as jnp
from jax import lax
from jax.sharding import Mesh
from jax.sharding import PartitionSpec as P

DP_EXPERT = ("dp", "expert_0", "expert_1", "expert_2")
EXPERT = ("expert_0", "expert_1", "expert_2")


def neutral_like(shard, identity):
    return jnp.zeros_like(shard) + jnp.asarray(identity, shard.dtype)


def carried_in(shard, axes, combine, identity):
    before = start = neutral_like(shard, identity)
    total = shard
    for axis in reversed(axes):
        length, here = (lax.axis_size(axis), lax.axis_index(axis))
        pieces = lax.all_gather(total, axis)
        inside, total = (start, start)
        for k in range(length):
            passed = k < here
            total = combine(total, pieces[k])
            inside = jnp.where(passed, total, inside)
        before = combine(inside, before)
    return before


def gather_turned(arrays, axis, dims):
    turned = [jnp.moveaxis(a, dim, 0) for a, dim in zip(arrays, dims)]
    both = jnp.concatenate([t.reshape(len(t), -1) for t in turned], axis=1)
    filled, at, finished = (lax.all_gather(both, axis, axis=0, tiled=True), 0, [])
    for t, dim in zip(turned, dims):
        piece = filled[:, at : at + t[0].size].reshape(-1, *t.shape[1:])
        finished.append(jnp.moveaxis(piece, 0, dim))
        at += t[0].size
    return tuple(finished)


def expert_rows(rows, gate_w, up_w, down_w):
    gate = jnp.dot(rows, gate_w, preferred_element_type=jnp.float32)
    up = jnp.dot(rows, up_w, preferred_element_type=jnp.float32)
    hidden = (jax.nn.silu(gate) * up).astype(jnp.bfloat16)
    return lax.dot_general(
        hidden, down_w, (((1,), (1,)), ((), ())), preferred_element_type=jnp.float32
    )


def add_counts(earlier, later):
    return earlier + later


def local(tokens, expert_ids, gate_units, capacity, w_gate, w_up, w_down):
    tok_rows = tokens.shape[0]
    width = tokens.shape[1]
    n_experts = capacity.shape[0]
    most = max(2, 5 * tok_rows // (2 * n_experts))
    slots_all = n_experts * most
    flat = expert_ids.reshape(-1)
    onehot = (flat[:, None] == jnp.arange(n_experts, dtype=jnp.int32)[None, :]).astype(jnp.int32)
    local_rank = jnp.sum((jnp.cumsum(onehot, axis=0) - onehot) * onehot, axis=1)
    counts = jnp.sum(onehot, axis=0)
    offsets = carried_in(counts, DP_EXPERT, add_counts, jnp.zeros_like(counts))
    global_slot = jnp.sum(onehot * offsets[None, :], axis=1) + local_rank
    limit = jnp.sum(onehot * capacity[None, :], axis=1)
    kept = global_slot < limit
    weight = jnp.where(kept, gate_units.reshape(-1).astype(jnp.float32) / 1024.0, jnp.float32(0.0))
    send_slot = flat * most + local_rank
    chosen = (send_slot[None, :] == jnp.arange(slots_all, dtype=jnp.int32)[:, None]) & kept[None, :]
    placing = jnp.sum(chosen.reshape(slots_all, tok_rows, 2).astype(jnp.int32), axis=2).astype(
        jnp.bfloat16
    )
    outgoing = jnp.dot(placing, tokens, preferred_element_type=jnp.float32).astype(jnp.bfloat16)
    outgoing = outgoing.reshape(n_experts, most, width)
    arrived = lax.all_to_all(outgoing, EXPERT, split_axis=0, concat_axis=0, tiled=True).reshape(
        slots_all, width
    )
    pieces = gather_turned((w_gate, w_up, w_down), "dp", (2, 2, 2))
    produced = expert_rows(arrived, pieces[0][0], pieces[1][0], pieces[2][0])
    answer = produced.astype(jnp.bfloat16).reshape(n_experts, most, width)
    back = lax.all_to_all(answer, EXPERT, split_axis=0, concat_axis=0, tiled=True).reshape(
        slots_all, width
    )
    picked = back[send_slot].astype(jnp.float32) * weight[:, None]
    mixed = jnp.sum(picked.reshape(tok_rows, 2, width), axis=1)
    return mixed.astype(jnp.bfloat16)


def solution(mesh):
    finer = Mesh(
        mesh.devices.reshape(mesh.shape["dp"], 8, 4, 2), ("dp", "expert_0", "expert_1", "expert_2")
    )
    return jax.shard_map(
        local,
        mesh=finer,
        in_specs=(
            P(DP_EXPERT, None),
            P(DP_EXPERT, None),
            P(DP_EXPERT, None),
            P(),
            P(EXPERT, None, "dp"),
            P(EXPERT, None, "dp"),
            P(EXPERT, None, "dp"),
        ),
        out_specs=P(DP_EXPERT, None),
        check_vma=False,
    )
```

profile of v0, /device:TPU:8, one launch (start us, length us, event | category | flops | bytes accessed | tf_op | source)
XLA Modules:
  0.0 272.6 jit_solution(670092717847320149)
XLA Ops:
  6.5 3.8 %pad_maximum_fusion = bf16[352,6144]{1,0:T(8,128)(2,1)} fusion(bf16[352,2048]{1,0:T(8,128)(2,1)} %bitcast.106, bf16[352,2048]{1,0:T(8,128)(2,1)} %bitcast.107, bf16[352,2048]{1,0:T(8,128)(2,1)} %bitcast.108), kind=kLoop, calls=%fused_computation.7 | loop fusion | flops 12976128 | bytes 8650752 | tf_op jit(solution)/shard_map/concatenate | solution.py:32
  10.5 0.6 copy-done.1
  11.5 0.6 dynamic-slice.1
  12.1 0.7 dynamic-slice
  14.1 0.6 reduce-window.6
  15.1 0.2 dynamic-update-slice
  15.3 1.8 all-reduce
  17.3 8.2 %all-reduce.1 = s32[256]{0:T(256)S(1)} all-reduce(s32[256]{0:T(256)S(1)} %fusion.26), channel_id=3, replica_groups=mesh['dp'=4,'expert_0'=8,'expert_1'=4,'expert_2'=2] {'expert_1'}, use_global_device_ids=true, to_apply=%add.1 | all-reduce | flops 256 | bytes 2048
  25.5 19.1 %all-gather.2 = s32[8,1,64]{2,1,0:T(1,128)S(1)} all-gather(s32[1,1,64]{2,1,0:T(1,128)S(1)} %fusion.32), channel_id=1, replica_groups=mesh['dp'=4,'expert_0'=8,'expert_1'=4,'expert_2'=2] {'expert_0'}, dimensions={0}, use_global_device_ids=true | all-gather | bytes 2304 | tf_op jit(solution)/shard_map/all_gather | solution.py:20
  44.7 10.0 %all-gather.3 = s32[4,1,64]{2,1,0:T(1,128)S(1)} all-gather(s32[1,1,64]{2,1,0:T(1,128)S(1)} %bitcast.110), channel_id=1, replica_groups=mesh['dp'=4,'expert_0'=8,'expert_1'=4,'expert_2'=2] {'dp'}, dimensions={0}, use_global_device_ids=true | all-gather | bytes 1280 | tf_op jit(solution)/shard_map/all_gather | solution.py:20
  55.7 1.6 convolution_convert_fusion
  57.3 2.4 reshape.138
  59.7 57.2 %all_to_all.10 = bf16[64,5,2048]{2,1,0:T(8,128)(2,1)} all-to-all(bf16[64,5,2048]{2,1,0:T(8,128)(2,1)S(1)} %reshape.138), channel_id=1, replica_groups=mesh['dp'=4,'expert_0'=8,'expert_1'=4,'expert_2'=2] {'expert_0','expert_..., dimensions={0} | all-to-all | bytes 2621440 | tf_op jit(solution)/shard_map/all_to_all | solution.py:76
  116.8 2.6 reshape.139
  119.4 56.2 %all-gather.6.cloned.1.call-done = bf16[1408,6144]{1,0:T(8,128)(2,1)} async-done(((bf16[352,6144]{1,0:T(8,128)(2,1)}), bf16[1408,6144]{1,0:T(8,128)(2,1)}) %all-gather.6.cloned.1.call-update) | async-done | bytes 17301520 | tf_op jit(solution)/shard_map/all_gather | solution.py:33
  175.6 6.1 %fusion.2 = f32[320,1408]{1,0:T(8,128)} fusion(bf16[320,2048]{1,0:T(8,128)(2,1)S(1)} %reshape.139, bf16[1408,6144]{1,0:T(8,128)(2,1)} %all-gather.6.cloned.1.call-done), kind=kOutput, calls=%fused_computation.6 | convolution fusion | flops 1845493760 | bytes 8880128 | tf_op jit(solution)/shard_map/dot_general | solution.py:42
  181.7 9.2 %fusion.4 = bf16[320,2048]{1,0:T(8,128)(2,1)S(1)} fusion(bf16[1408,6144]{1,0:T(8,128)(2,1)} %all-gather.6.cloned.1.call-done, bf16[320,2048]{1,0:T(8,128)(2,1)S(1)} %reshape.139, f32[320,1408]{1,0:T(8,128)} %fusion.2), kind=kOutput, calls=%fused_computation.9 | convolution fusion | flops 3694346240 | bytes 15958016 | tf_op jit(solution)/shard_map/dot_general | solution.py:45
  190.9 1.6 reshape.146
  192.5 10.8 %all-to-all-start.1 = ((bf16[64,5,2048]{2,1,0:T(8,128)(2,1)}), bf16[64,5,2048]{2,1,0:T(8,128)(2,1)}, u32[]{:S(2)}, u32[]{:S(2)}) async-start(bf16[64,5,2048]{2,1,0:T(8,128)(2,1)} %reshape.146), calls=%async_computation.1 | async-start | bytes 4194304 | tf_op jit(solution)/shard_map/all_to_all | solution.py:82
  203.5 50.9 %all-to-all-done.1 = bf16[64,5,2048]{2,1,0:T(8,128)(2,1)} async-done(((bf16[64,5,2048]{2,1,0:T(8,128)(2,1)}), bf16[64,5,2048]{2,1,0:T(8,128)(2,1)}, u32[]{:S(2)}, u32[]{:S(2)}) %all-to-all-start.1) | async-done | bytes 1310752 | tf_op jit(solution)/shard_map/all_to_all | solution.py:82
  254.4 2.6 reshape.147
  256.9 2.3 gather_fusion
  259.3 2.4 reshape.148
  261.7 4.0 %multiply_reduce_fusion = bf16[128,2048]{1,0:T(8,128)(2,1)} fusion(f32[128,2,2048]{2,1,0:T(2,128)S(1)} %reshape.148, f32[128,2]{1,0:T(8,128)S(1)} %copy.39), kind=kLoop, calls=%fused_computation.12 | loop fusion | flops 786432 | bytes 2622464 | tf_op jit(solution)/shard_map/reduce_sum | solution.py:86
  (42 shorter events, 2.3 us)
Async XLA Ops:
  6.5 49.1 %copy-start = (bf16[128,2048]{1,0:T(8,128)(2,1)S(1)}, bf16[128,2048]{1,0:T(8,128)(2,1)}, u32[]{:S(2)}) copy-start(bf16[128,2048]{1,0:T(8,128)(2,1)} %param.7) | copy-start | bytes 1572868
  6.5 169.1 %all-gather.6.cloned.1.call-start = ((), (), s32[]{:S(2)}) async-start(), calls=%async_computation.2 | async-start | bytes 21626880 | tf_op jit(solution)/shard_map/all_gather | solution.py:33
  10.4 0.7 copy-start.1
  10.4 1.1 copy-start.5
  10.4 1.7 copy-start.4
  10.4 44.3 %copy-start.3 = (s32[64]{0:T(128)S(1)}, s32[64]{0:T(128)}, u32[]{:S(2)}) copy-start(s32[64]{0:T(128)} %param.10) | copy-start | bytes 772
  10.4 45.2 %copy-start.2 = (s32[128,2]{0,1:T(2,128)S(1)}, s32[128,2]{0,1:T(2,128)}, u32[]{:S(2)}) copy-start(s32[128,2]{0,1:T(2,128)} %param.9) | copy-start | bytes 3076
  192.5 61.9 %all-to-all-start.1 = ((bf16[64,5,2048]{2,1,0:T(8,128)(2,1)}), bf16[64,5,2048]{2,1,0:T(8,128)(2,1)}, u32[]{:S(2)}, u32[]{:S(2)}) async-start(bf16[64,5,2048]{2,1,0:T(8,128)(2,1)} %reshape.146), calls=%async_computation.1 | async-start | bytes 4194304 | tf_op jit(solution)/shard_map/all_to_all | solution.py:82
Sparse Core Ops, SparseCore 0:
  10.6 164.9 all-gather.5
where the time goes:
time: 273 us
  waiting for transfers between devices  107 us (39%)
  blocking collectives  96.3 us (35%)
  local copies, waits for them, and re-layouts  17.4 us (6%)
  matrix products  16.9 us (6%)
  between operations  15 us (5%)
  starting transfers between devices  10.8 us (4%)
  other arithmetic  9.2 us (3%)
    all_to_all x1, blocking collectives, local(): lax.all_to_all(outgoing, EXPERT, split_axis=0, concat_axis=0, tiled=True)  57.2 us
    all_gather x1, waiting for transfers between devices, gather_turned(): lax.all_gather(both, axis, axis=0, tiled=True)  56.2 us
    all_to_all x1, waiting for transfers between devices, local(): lax.all_to_all(answer, EXPERT, split_axis=0, concat_axis=0, tiled=True)  50.9 us
    all_gather x2, blocking collectives, carried_in(): pieces = lax.all_gather(total, axis)  29.1 us
    all_to_all x1, starting transfers between devices, local(): lax.all_to_all(answer, EXPERT, split_axis=0, concat_axis=0, tiled=True)  10.8 us
    unnamed x2, blocking collectives  9.97 us
    dot_general x1, matrix products, expert_rows(): lax.dot_general(hidden, down_w, (((1,), (1,)), ((), ())), preferred_eleme...  9.2 us
    dot_general x1, matrix products, expert_rows(): gate = jnp.dot(rows, gate_w, preferred_element_type=jnp.float32)  6.1 us
  transfers between devices with their start and end apart: 2, of which 2 were waited for; matrix products, arithmetic and copies ran while one was open for 4% of the time, Pallas kernels for 0%

commit v1 on v0

--- a/solution.py
+++ b/solution.py
@@ -30,7 +30,13 @@
 def gather_turned(arrays, axis, dims):
     turned = [jnp.moveaxis(a, dim, 0) for a, dim in zip(arrays, dims)]
     both = jnp.concatenate([t.reshape(len(t), -1) for t in turned], axis=1)
-    filled, at, finished = (lax.all_gather(both, axis, axis=0, tiled=True), 0, [])
+    filled, at, finished = (
+        jnp.concatenate(
+            lax.all_to_all(jnp.stack([both] * lax.axis_size(axis)), axis, 0, 0), axis=0
+        ),
+        0,
+        [],
+    )
     for t, dim in zip(turned, dims):
         piece = filled[:, at : at + t[0].size].reshape(-1, *t.shape[1:])
         finished.append(jnp.moveaxis(piece, 0, dim))

time: 273 us -> 397 us (1.45)
  waiting for transfers between devices: 107 us -> 285 us
  blocking collectives: 96.3 us -> 38.8 us
  between operations: 15 us -> 1.51 us
  starting transfers between devices: 10.8 us -> 20.1 us
  local copies, waits for them, and re-layouts: 17.4 us -> 24.6 us
    all_to_all x0 -> x2, waiting for transfers between devices: none -> 234 us  [the longest x1 187 us: gather_turned(): lax.all_to_all(jnp.stack([both] * lax.axis_size(axis)), axis, 0, 0)]
    all_to_all x1 -> x0, blocking collectives: 57.2 us -> none  [local(): lax.all_to_all(outgoing, EXPERT, split_axis=0, concat_axis=0, tiled=True)]
    all_gather x1 -> x0, waiting for transfers between devices: 56.2 us -> none  [gather_turned(): lax.all_gather(both, axis, axis=0, tiled=True)]
    all_to_all x0 -> x2, starting transfers between devices: none -> 13.1 us  [the longest x1 7.06 us: gather_turned(): lax.all_to_all(jnp.stack([both] * lax.axis_size(axis)), axis, 0, 0)]
    another operation x1 -> x2, local copies, waits for them, and re-layouts: 0.01 us -> 7.65 us  [the longest x1 7.65 us: gather_turned(): jnp.stack([both] * lax.axis_size(axis))]
  transfers between devices with their start and end apart: 2 -> 3, of which waited for: 2 -> 3; matrix products, arithmetic and copies ran while one was open for 4% -> 1% of each run, Pallas kernels for 0% -> 0%
where the time goes in v1:
time: 397 us
  waiting for transfers between devices  285 us (72%)
  blocking collectives  38.8 us (10%)
  local copies, waits for them, and re-layouts  24.6 us (6%)
  starting transfers between devices  20.1 us (5%)
  matrix products  16.3 us (4%)
  other arithmetic  10.3 us (3%)
    all_to_all x1, waiting for transfers between devices, gather_turned(): lax.all_to_all(jnp.stack([both] * lax.axis_size(axis)), axis, 0, 0)  187 us
    all_to_all x1, waiting for transfers between devices, local(): lax.all_to_all(answer, EXPERT, split_axis=0, concat_axis=0, tiled=True)  50.9 us
    all_to_all x1, waiting for transfers between devices, local(): lax.all_to_all(outgoing, EXPERT, split_axis=0, concat_axis=0, tiled=True)  47.5 us
    all_gather x2, blocking collectives, carried_in(): pieces = lax.all_gather(total, axis)  28.8 us
    unnamed x2, blocking collectives  9.97 us
    dot_general x1, matrix products, expert_rows(): lax.dot_general(hidden, down_w, (((1,), (1,)), ((), ())), preferred_eleme...  9.2 us
  transfers between devices with their start and end apart: 3, of which 3 were waited for; matrix products, arithmetic and copies ran while one was open for 1% of the time, Pallas kernels for 0%

profile of v1, /device:TPU:8, one launch (start us, length us, event | category | flops | bytes accessed | tf_op | source)
XLA Modules:
  0.0 396.7 jit_solution(186294522271620228)
XLA Ops:
  0.0 0.8 copy.31
  1.2 1.3 dynamic-slice.1
  2.5 1.3 dynamic-slice
  5.4 1.8 all-reduce
  7.4 8.2 %all-reduce.1 = s32[256]{0:T(256)S(1)} all-reduce(s32[256]{0:T(256)S(1)} %fusion.26), channel_id=3, replica_groups=mesh['dp'=4,'expert_0'=8,'expert_1'=4,'expert_2'=2] {'expert_1'}, use_global_device_ids=true, to_apply=%add.1 | all-reduce | flops 256 | bytes 2048
  15.7 19.1 %all-gather.2 = s32[8,1,64]{2,1,0:T(1,128)S(1)} all-gather(s32[1,1,64]{2,1,0:T(1,128)S(1)} %fusion.32), channel_id=1, replica_groups=mesh['dp'=4,'expert_0'=8,'expert_1'=4,'expert_2'=2] {'expert_0'}, dimensions={0}, use_global_device_ids=true | all-gather | bytes 2304 | tf_op jit(solution)/shard_map/all_gather | solution.py:20
  34.8 9.7 %all-gather.3 = s32[4,1,64]{2,1,0:T(1,128)S(1)} all-gather(s32[1,1,64]{2,1,0:T(1,128)S(1)} %bitcast.111), channel_id=1, replica_groups=mesh['dp'=4,'expert_0'=8,'expert_1'=4,'expert_2'=2] {'dp'}, dimensions={0}, use_global_device_ids=true | all-gather | bytes 1280 | tf_op jit(solution)/shard_map/all_gather | solution.py:20
  48.2 1.6 reshape.143
  49.8 6.0 %all-to-all-start = ((bf16[64,5,2048]{2,1,0:T(8,128)(2,1)}), bf16[64,5,2048]{2,1,0:T(8,128)(2,1)S(1)}, u32[]{:S(2)}, u32[]{:S(2)}) async-start(bf16[64,5,2048]{2,1,0:T(8,128)(2,1)} %reshape.143), calls=%async_computation | async-start | bytes 4194304 | tf_op jit(solution)/shard_map/all_to_all | solution.py:82
  55.9 3.8 pad_maximum_fusion
  59.6 47.5 %all-to-all-done = bf16[64,5,2048]{2,1,0:T(8,128)(2,1)S(1)} async-done(((bf16[64,5,2048]{2,1,0:T(8,128)(2,1)}), bf16[64,5,2048]{2,1,0:T(8,128)(2,1)S(1)}, u32[]{:S(2)}, u32[]{:S(2)}) %all-to-all-start) | async-done | bytes 1310752 | tf_op jit(solution)/shard_map/all_to_all | solution.py:82
  107.1 7.6 %stack.2 = bf16[4,352,6144]{2,1,0:T(8,128)(2,1)} broadcast(bf16[352,6144]{1,0:T(8,128)(2,1)} %pad_maximum_fusion), dimensions={1,2} | broadcast | bytes 21626880 | tf_op jit(solution)/shard_map/stack | solution.py:35
  114.8 7.1 %all-to-all-start.1 = ((bf16[4,352,6144]{2,1,0:T(8,128)(2,1)}), bf16[4,352,6144]{2,1,0:T(8,128)(2,1)}, u32[]{:S(2)}, u32[]{:S(2)}) async-start(bf16[4,352,6144]{2,1,0:T(8,128)(2,1)} %stack.2), calls=%async_computation.1 | async-start | bytes 34603008 | tf_op jit(solution)/shard_map/all_to_all | solution.py:35
  121.8 1.4 reshape.144
  123.2 186.7 %all-to-all-done.1 = bf16[4,352,6144]{2,1,0:T(8,128)(2,1)} async-done(((bf16[4,352,6144]{2,1,0:T(8,128)(2,1)}), bf16[4,352,6144]{2,1,0:T(8,128)(2,1)}, u32[]{:S(2)}, u32[]{:S(2)}) %all-to-all-start.1) | async-done | bytes 17301536 | tf_op jit(solution)/shard_map/all_to_all | solution.py:35
  309.9 6.6 %fusion.2 = f32[320,1408]{1,0:T(8,128)} fusion(bf16[320,2048]{1,0:T(8,128)(2,1)} %reshape.144, bf16[1408,6144]{1,0:T(8,128)(2,1)} %bitcast.21), kind=kOutput, calls=%fused_computation.6 | convolution fusion | flops 1845493760 | bytes 8880128 | tf_op jit(solution)/shard_map/dot_general | solution.py:48
  316.5 9.2 %fusion.4 = bf16[320,2048]{1,0:T(8,128)(2,1)S(1)} fusion(bf16[1408,6144]{1,0:T(8,128)(2,1)} %bitcast.21, bf16[320,2048]{1,0:T(8,128)(2,1)S(1)} %copy-done.1, f32[320,1408]{1,0:T(8,128)} %fusion.2), kind=kOutput, calls=%fused_computation.9 | convolution fusion | flops 3694346240 | bytes 15958016 | tf_op jit(solution)/shard_map/dot_general | solution.py:51
  325.7 1.6 reshape.152
  327.3 7.0 %all-to-all-start.2 = ((bf16[64,5,2048]{2,1,0:T(8,128)(2,1)}), bf16[64,5,2048]{2,1,0:T(8,128)(2,1)}, u32[]{:S(2)}, u32[]{:S(2)}) async-start(bf16[64,5,2048]{2,1,0:T(8,128)(2,1)} %reshape.152), calls=%async_computation.2 | async-start | bytes 4194304 | tf_op jit(solution)/shard_map/all_to_all | solution.py:88
  334.6 50.9 %all-to-all-done.2 = bf16[64,5,2048]{2,1,0:T(8,128)(2,1)} async-done(((bf16[64,5,2048]{2,1,0:T(8,128)(2,1)}), bf16[64,5,2048]{2,1,0:T(8,128)(2,1)}, u32[]{:S(2)}, u32[]{:S(2)}) %all-to-all-start.2) | async-done | bytes 1310752 | tf_op jit(solution)/shard_map/all_to_all | solution.py:88
  385.5 2.6 reshape.153
  388.0 2.3 gather_fusion
  390.4 2.4 reshape.154
  392.7 3.9 multiply_reduce_fusion
  (35 shorter events, 4.8 us)
Async XLA Ops:
  0.0 47.7 %copy-start = (bf16[128,2048]{1,0:T(8,128)(2,1)S(1)}, bf16[128,2048]{1,0:T(8,128)(2,1)}, u32[]{:S(2)}) copy-start(bf16[128,2048]{1,0:T(8,128)(2,1)} %param.7) | copy-start | bytes 1572868
  49.8 57.3 %all-to-all-start = ((bf16[64,5,2048]{2,1,0:T(8,128)(2,1)}), bf16[64,5,2048]{2,1,0:T(8,128)(2,1)S(1)}, u32[]{:S(2)}, u32[]{:S(2)}) async-start(bf16[64,5,2048]{2,1,0:T(8,128)(2,1)} %reshape.143), calls=%async_computation | async-start | bytes 4194304 | tf_op jit(solution)/shard_map/all_to_all | solution.py:82
  114.8 195.1 %all-to-all-start.1 = ((bf16[4,352,6144]{2,1,0:T(8,128)(2,1)}), bf16[4,352,6144]{2,1,0:T(8,128)(2,1)}, u32[]{:S(2)}, u32[]{:S(2)}) async-start(bf16[4,352,6144]{2,1,0:T(8,128)(2,1)} %stack.2), calls=%async_computation.1 | async-start | bytes 34603008 | tf_op jit(solution)/shard_map/all_to_all | solution.py:35
  309.9 6.6 %copy-start.1 = (bf16[320,2048]{1,0:T(8,128)(2,1)S(1)}, bf16[320,2048]{1,0:T(8,128)(2,1)}, u32[]{:S(2)}) copy-start(bf16[320,2048]{1,0:T(8,128)(2,1)} %reshape.144) | copy-start | bytes 3932164
  327.3 58.2 %all-to-all-start.2 = ((bf16[64,5,2048]{2,1,0:T(8,128)(2,1)}), bf16[64,5,2048]{2,1,0:T(8,128)(2,1)}, u32[]{:S(2)}, u32[]{:S(2)}) async-start(bf16[64,5,2048]{2,1,0:T(8,128)(2,1)} %reshape.152), calls=%async_computation.2 | async-start | bytes 4194304 | tf_op jit(solution)/shard_map/all_to_all | solution.py:88
